TPU v7x, 32 devices: a whole 2x2x4 slice. The times are simulated.
32 devices in a mesh: shard: 4 (over y, x), cols: 8 (over z, core).
Axes of the slice: x: 2, y: 2, z: 4, core: 2. Of those that a mesh axis runs over, the one named last changes fastest.
Arguments:
- train_gate: bfloat16 [4096, 14336], P('shard', 'cols'), may hold values from -0.09375 to 0.09375
- low_gate: bfloat16 [4096, 32], P('shard'), may hold values from -0.09375 to 0.09375
- high_gate: bfloat16 [32, 14336], P(None, 'cols'), may hold values from -1 to 1
- train_up: bfloat16 [4096, 14336], P('shard', 'cols'), may hold values from -0.09375 to 0.09375
- low_up: bfloat16 [4096, 32], P('shard'), may hold values from -0.09375 to 0.09375
- high_up: bfloat16 [32, 14336], P(None, 'cols'), may hold values from -1 to 1
- norm_train: float32 [4096], P(('shard', 'cols')), may hold values from 0.25 to 1.75
- norm_step: float32 [4096], P(('shard', 'cols')), may hold values from -0.3 to 0.3
Outputs:
- ready_gate: bfloat16 [14336, 4096], P('cols')
- ready_up: bfloat16 [14336, 4096], P('cols')
- serve_norm: bfloat16 [4096], replicated
All inputs are finite; a program needn't handle non-finite values.
Results may differ from a plain program's by a relative error of at most 0.001.
Values may be sent and summed in bfloat16 or wider, within the bound.
A program may use at most 128 MiB of HBM per device.

v0:
```python
import functools

import jax
import jax.numpy as jnp
from jax import lax
from jax.experimental import pallas as pl
from jax.experimental.pallas import tpu as pltpu
from jax.sharding import PartitionSpec as P


mix_rate = 1.0
TILE = 256
GRANT = 60 << 20


def chunks_of(width):
    cuts, at = [], 0
    while at < width:
        size = min(TILE if at == 0 else 2 * TILE, width - at)
        cuts.append((at, size))
        at += size
    return cuts


def merge_body(*refs):
    for train_ref, low_ref, high_ref, out_ref in (refs[0:3] + refs[6:7], refs[3:6] + refs[7:8]):
        update = lax.dot_general(
            low_ref[...], high_ref[...], (((0,), (0,)), ((), ())), preferred_element_type=jnp.float32
        )
        latest = train_ref[...].astype(jnp.float32) + mix_rate * update
        out_ref[...] = latest.astype(jnp.bfloat16).T


def merge(weights, start, size):
    train, low, _ = weights[0]
    rows, rank = train.shape[0], low.shape[0]
    first = start // TILE
    in_specs = [
        pl.BlockSpec((rows, TILE), lambda j: (0, first + j)),
        pl.BlockSpec((rank, rows), lambda j: (0, 0)),
        pl.BlockSpec((rank, TILE), lambda j: (0, first + j)),
    ] * 2
    return pl.pallas_call(
        merge_body,
        grid=(size // TILE,),
        in_specs=in_specs,
        out_specs=[pl.BlockSpec((TILE, rows), lambda j: (j, 0))] * 2,
        out_shape=[jax.ShapeDtypeStruct((size, rows), jnp.bfloat16)] * 2,
        compiler_params=pltpu.CompilerParams(vmem_limit_bytes=GRANT),
        cost_estimate=pl.CostEstimate(
            flops=4 * rows * rank * size, bytes_accessed=8 * rows * size, transcendentals=0
        ),
    )(*weights[0], *weights[1])


def place_body(jobs, aliased, *refs):
    n = len(jobs)
    pieces, outs = refs[:n], refs[n + aliased : n + aliased + 2]
    bufs, get_sem, put_sem = refs[n + aliased + 2 : -2], refs[-2], refs[-1]
    me = lax.axis_index("shard")
    bit0, bit1 = lax.rem(me, 2), me // 2
    gets, puts = [], []
    for k, (which, start, size, flip) in enumerate(jobs):
        cols = pieces[k].shape[1]
        source = (1 - bit1 if flip & 2 else bit1) * 2 + (1 - bit0 if flip & 1 else bit0)
        at = pl.multiple_of(source * cols, cols)
        gets.append(pltpu.make_async_copy(pieces[k], bufs[k], get_sem.at[k]))
        puts.append(
            pltpu.make_async_copy(
                bufs[k], outs[which].at[pl.ds(start, size), pl.ds(at, cols)], put_sem.at[k]
            )
        )
    for get in gets:
        get.start()
    for get, put in zip(gets, puts):
        get.wait()
        put.start()
    for put in puts:
        put.wait()


def place(outs, shape, pieces, jobs):
    any_spec = pl.BlockSpec(memory_space=pl.ANY)
    aliased = len(outs)
    n = len(pieces)
    moved = sum(2 * 2 * p.size for p in pieces)
    return pl.pallas_call(
        functools.partial(place_body, jobs, aliased),
        in_specs=[any_spec] * (n + aliased),
        out_specs=[any_spec] * 2,
        out_shape=[jax.ShapeDtypeStruct(shape, jnp.bfloat16)] * 2,
        scratch_shapes=[pltpu.VMEM(p.shape, jnp.bfloat16) for p in pieces]
        + [pltpu.SemaphoreType.DMA((n,)), pltpu.SemaphoreType.DMA((n,))],
        input_output_aliases={n: 0, n + 1: 1} if aliased else {},
        compiler_params=pltpu.CompilerParams(vmem_limit_bytes=GRANT),
        cost_estimate=pl.CostEstimate(flops=0, bytes_accessed=moved, transcendentals=0),
    )(*pieces, *outs)


def last_order(cuts):
    return list(range(1, len(cuts))) + [0]


def hop(n, step, piece):
    return lax.ppermute(piece, "shard", perm=[(i, i ^ step) for i in range(n)])


def exchange(n, weights):
    rows, width = weights[0][0].shape
    cuts = chunks_of(width)
    span = range(len(cuts))
    gate, up = [], []
    for k in span:
        g, u = merge(weights, *cuts[k])
        gate.append(g)
        up.append(u)
    gate_x = [hop(n, 1, gate[k]) for k in span]
    up_y = [hop(n, 2, up[k]) for k in span]
    up_x = [hop(n, 1, up[k]) for k in span]
    gate_y = [hop(n, 2, gate[k]) for k in span]
    up_d = [hop(n, 1, up_y[k]) for k in span]
    gate_d = [hop(n, 2, gate_x[k]) for k in span]
    stages = [
        [(gate[k], (0, *cuts[k], 0)) for k in span] + [(up[k], (1, *cuts[k], 0)) for k in span],
        [p for k in span for p in ((gate_x[k], (0, *cuts[k], 1)), (up_y[k], (1, *cuts[k], 2)))],
        [p for k in span for p in ((gate_y[k], (0, *cuts[k], 2)), (up_x[k], (1, *cuts[k], 1)))],
    ]
    for k in last_order(cuts):
        stages.append([(gate_d[k], (0, *cuts[k], 3)), (up_d[k], (1, *cuts[k], 3))])
    outs = ()
    for stage in stages:
        outs = place(outs, (width, n * rows), [p for p, _ in stage], tuple(j for _, j in stage))
    return outs


def fits(n, rows, width):
    return n == 4 and width % TILE == 0 and rows % 128 == 0


def per_device(n, train_gate, low_gate, high_gate, train_up, low_up, high_up, norm_train, norm_step):
    serve_norm = lax.all_gather((norm_train + norm_step).astype(jnp.bfloat16), ("shard", "cols"), axis=0, tiled=True)
    if fits(n, *train_gate.shape):
        ready_gate, ready_up = exchange(
            n, ((train_gate, low_gate.T, high_gate), (train_up, low_up.T, high_up))
        )
    else:
        ready = []
        for train, low, high in ((train_gate, low_gate, high_gate), (train_up, low_up, high_up)):
            latest = train.astype(jnp.float32) + mix_rate * jnp.dot(
                low, high, preferred_element_type=jnp.float32
            )
            ready.append(lax.all_gather(latest.astype(jnp.bfloat16), "shard", axis=0, tiled=True).T)
        ready_gate, ready_up = ready
    return (ready_gate, ready_up, serve_norm)


def solution(mesh):
    n = mesh.shape["shard"]
    step = jax.shard_map(
        functools.partial(per_device, n),
        mesh=mesh,
        in_specs=(
            P("shard", "cols"),
            P("shard", None),
            P(None, "cols"),
            P("shard", "cols"),
            P("shard", None),
            P(None, "cols"),
            P(("shard", "cols")),
            P(("shard", "cols")),
        ),
        out_specs=(P("cols", None), P("cols", None), P()),
        check_vma=False,
    )

    def whole(train_gate, *rest):
        rows, width = train_gate.shape[0] // n, train_gate.shape[1] // mesh.shape["cols"]
        run = step
        if fits(n, rows, width):
            run = step
        return run(train_gate, *rest)

    return whole
```

profile of v0, /device:TPU:0, one launch (start us, length us, event | category | flops | bytes accessed | tf_op | source)
XLA Modules:
  0.0 282.4 jit_solution(3586688833616105517)
XLA Ops:
  0.6 2.8 shard_map.103
  3.4 3.0 %collective-permute-start = (bf16[256,1024]{1,0:T(8,128)(2,1)}, bf16[256,1024]{1,0:T(8,128)(2,1)}, u32[]{:S(2)}, u32[]{:S(2)}) collective-permute-start(bf16[256,1024]{1,0:T(8,128)(2,1)} %get-tuple-element.25.refs_0_), channel_id=1, source_target_pairs={{0,8},{8,0},{16,24},{24,16},{1,9},{9,1},{17,25},{25,17},{2,10},{10... | collective-permute-start | bytes 1572872 | tf_op jit(solution)/shard_map/ppermute | solution.py:105
  6.4 1.5 collective-permute-start.2
  8.4 3.4 %shard_map.105 = (bf16[512,1024]{1,0:T(8,128)(2,1)}, bf16[512,1024]{1,0:T(8,128)(2,1)}) custom-call(bf16[1024,1792]{1,0:T(8,128)(2,1)} %refs_0_.7, bf16[32,1024]{1,0:T(8,128)(2,1)} %bitcast.6, bf16[32,1792]{1,0:T(8,128)(2,1)} %refs_2_.7, bf16[1024,1792]{1,0:T(8,128)(2,1)} %refs_3_.7, bf16[32,1024]{1,0:T(8,128)(2,1)} %bitcast.10, bf16[32,1792]{1,0:T(8,128)(2,1)} %refs_5_.7), custom_call_target="tpu_custom_call" | custom-call | flops 67108864 | bytes 4194304 | tf_op jit(solution)/shard_map/pallas_call | solution.py:43
  11.9 1.5 collective-permute-start.10
  13.4 3.4 %shard_map.106 = (bf16[512,1024]{1,0:T(8,128)(2,1)}, bf16[512,1024]{1,0:T(8,128)(2,1)}) custom-call(bf16[1024,1792]{1,0:T(8,128)(2,1)} %refs_0_.7, bf16[32,1024]{1,0:T(8,128)(2,1)} %bitcast.7, bf16[32,1792]{1,0:T(8,128)(2,1)} %refs_2_.7, bf16[1024,1792]{1,0:T(8,128)(2,1)} %refs_3_.7, bf16[32,1024]{1,0:T(8,128)(2,1)} %bitcast.11, bf16[32,1792]{1,0:T(8,128)(2,1)} %refs_5_.7), custom_call_target="tpu_custom_call" | custom-call | flops 67108864 | bytes 4194304 | tf_op jit(solution)/shard_map/pallas_call | solution.py:43
  17.3 1.7 collective-permute-done.refs_0_
  19.0 2.5 collective-permute-start.14
  23.0 3.4 %shard_map.104 = (bf16[512,1024]{1,0:T(8,128)(2,1)}, bf16[512,1024]{1,0:T(8,128)(2,1)}) custom-call(bf16[1024,1792]{1,0:T(8,128)(2,1)} %refs_0_.7, bf16[32,1024]{1,0:T(8,128)(2,1)} %bitcast.8, bf16[32,1792]{1,0:T(8,128)(2,1)} %refs_2_.7, bf16[1024,1792]{1,0:T(8,128)(2,1)} %refs_3_.7, bf16[32,1024]{1,0:T(8,128)(2,1)} %bitcast.12, bf16[32,1792]{1,0:T(8,128)(2,1)} %refs_5_.7), custom_call_target="tpu_custom_call" | custom-call | flops 67108864 | bytes 4194304 | tf_op jit(solution)/shard_map/pallas_call | solution.py:43
  26.5 6.2 %collective-permute-done.16.refs_0_ = bf16[256,1024]{1,0:T(8,128)(2,1)S(1)} collective-permute-done((bf16[256,1024]{1,0:T(8,128)(2,1)}, bf16[256,1024]{1,0:T(8,128)(2,1)S(1)}, u32[]{:S(2)}, u32[]{:S(2)}) %collective-permute-start.16) | collective-permute-done | bytes 524320 | tf_op jit(solution)/shard_map/ppermute | solution.py:105
  33.5 20.7 %collective-permute-done.17.refs_1_ = bf16[256,1024]{1,0:T(8,128)(2,1)S(1)} collective-permute-done((bf16[256,1024]{1,0:T(8,128)(2,1)S(1)}, bf16[256,1024]{1,0:T(8,128)(2,1)S(1)}, u32[]{:S(2)}, u32[]{:S(2)}) %collective-permute-start.17) | collective-permute-done | bytes 524320 | tf_op jit(solution)/shard_map/ppermute | solution.py:105
  58.0 19.7 %collective-permute-done.14.refs_3_ = bf16[512,1024]{1,0:T(8,128)(2,1)} collective-permute-done((bf16[512,1024]{1,0:T(8,128)(2,1)}, bf16[512,1024]{1,0:T(8,128)(2,1)}, u32[]{:S(2)}, u32[]{:S(2)}) %collective-permute-start.14) | collective-permute-done | bytes 1048608 | tf_op jit(solution)/shard_map/ppermute | solution.py:105
  77.8 2.0 collective-permute-start.20
  79.8 20.3 %collective-permute-done.6.refs_7_ = bf16[512,1024]{1,0:T(8,128)(2,1)S(1)} collective-permute-done((bf16[512,1024]{1,0:T(8,128)(2,1)}, bf16[512,1024]{1,0:T(8,128)(2,1)S(1)}, u32[]{:S(2)}, u32[]{:S(2)}) %collective-permute-start.6) | collective-permute-done | bytes 1048608 | tf_op jit(solution)/shard_map/ppermute | solution.py:105
  100.2 2.0 collective-permute-start.22
  102.1 20.4 %collective-permute-done.18.refs_2_ = bf16[512,1024]{1,0:T(8,128)(2,1)S(1)} collective-permute-done((bf16[512,1024]{1,0:T(8,128)(2,1)}, bf16[512,1024]{1,0:T(8,128)(2,1)S(1)}, u32[]{:S(2)}, u32[]{:S(2)}) %collective-permute-start.18) | collective-permute-done | bytes 1048608 | tf_op jit(solution)/shard_map/ppermute | solution.py:105
  122.6 2.0 collective-permute-start.13
  124.6 20.4 %collective-permute-done.20.refs_4_ = bf16[512,1024]{1,0:T(8,128)(2,1)S(1)} collective-permute-done((bf16[512,1024]{1,0:T(8,128)(2,1)}, bf16[512,1024]{1,0:T(8,128)(2,1)S(1)}, u32[]{:S(2)}, u32[]{:S(2)}) %collective-permute-start.20) | collective-permute-done | bytes 1048608 | tf_op jit(solution)/shard_map/ppermute | solution.py:105
  145.1 1.9 collective-permute-start.11
  147.0 20.4 %collective-permute-done.22.refs_6_ = bf16[512,1024]{1,0:T(8,128)(2,1)S(1)} collective-permute-done((bf16[512,1024]{1,0:T(8,128)(2,1)}, bf16[512,1024]{1,0:T(8,128)(2,1)S(1)}, u32[]{:S(2)}, u32[]{:S(2)}) %collective-permute-start.22) | collective-permute-done | bytes 1048608 | tf_op jit(solution)/shard_map/ppermute | solution.py:105
  167.5 1.5 collective-permute-start.9
  169.5 20.4 %collective-permute-done.13.refs_0_ = bf16[512,1024]{1,0:T(8,128)(2,1)S(1)} collective-permute-done((bf16[512,1024]{1,0:T(8,128)(2,1)}, bf16[512,1024]{1,0:T(8,128)(2,1)S(1)}, u32[]{:S(2)}, u32[]{:S(2)}) %collective-permute-start.13) | collective-permute-done | bytes 1048608 | tf_op jit(solution)/shard_map/ppermute | solution.py:105
  190.0 2.0 collective-permute-start.1
  192.0 19.6 %collective-permute-done.11.refs_1_ = bf16[512,1024]{1,0:T(8,128)(2,1)S(1)} collective-permute-done((bf16[512,1024]{1,0:T(8,128)(2,1)S(1)}, bf16[512,1024]{1,0:T(8,128)(2,1)S(1)}, u32[]{:S(2)}, u32[]{:S(2)}) %collective-permute-start.11) | collective-permute-done | bytes 1048608 | tf_op jit(solution)/shard_map/ppermute | solution.py:105
  213.4 5.9 %shard_map.107 = (bf16[1792,4096]{1,0:T(8,128)(2,1)}, bf16[1792,4096]{1,0:T(8,128)(2,1)}) custom-call(bf16[256,1024]{1,0:T(8,128)(2,1)} %get-tuple-element.25.refs_0_, bf16[512,1024]{1,0:T(8,128)(2,1)} %get-tuple-element.31.refs_1_, bf16[512,1024]{1,0:T(8,128)(2,1)} %get-tuple-element.29.refs_2_, bf16[512,1024]{1,0:T(8,128)(2,1)} %get-tuple-element.27.refs_3_, ...), custom_call_target="tpu_custom_call" | custom-call | bytes 14680064 | tf_op jit(solution)/shard_map/pallas_call | solution.py:87
  219.4 40.9 %all-gather = bf16[32,1,128]{2,1,0:T(2,128)(2,1)S(1)} all-gather(bf16[1,1,128]{2,1,0:T(2,128)(2,1)S(1)} %convert_bitcast_fusion), channel_id=1, replica_groups=mesh['shard'=4,'cols'=8] {'shard','cols'}, dimensions={0}, use_global_device_ids=true | all-gather | bytes 8448 | tf_op jit(solution)/shard_map/all_gather | solution.py:141
  261.0 5.8 %shard_map.108 = (bf16[1792,4096]{1,0:T(8,128)(2,1)}, bf16[1792,4096]{1,0:T(8,128)(2,1)}) custom-call(bf16[256,1024]{1,0:T(8,128)(2,1)} %collective-permute-done.refs_0_, bf16[256,1024]{1,0:T(8,128)(2,1)} %collective-permute-done.2.refs_1_, bf16[512,1024]{1,0:T(8,128)(2,1)} %collective-permute-done.12.refs_2_, ...), custom_call_target="tpu_custom_call", output_to_operand_aliasing={{0}: (8, {}), {1}: (9, {})} | custom-call | bytes 14680064 | tf_op jit(solution)/shard_map/pallas_call | solution.py:87
  266.8 5.8 %shard_map.109 = (bf16[1792,4096]{1,0:T(8,128)(2,1)}, bf16[1792,4096]{1,0:T(8,128)(2,1)}) custom-call(bf16[256,1024]{1,0:T(8,128)(2,1)} %copy-done.12, bf16[256,1024]{1,0:T(8,128)(2,1)} %copy-done.13, bf16[512,1024]{1,0:T(8,128)(2,1)} %copy-done.3, bf16[512,1024]{1,0:T(8,128)(2,1)} %copy-done.4, ...), custom_call_target="tpu_custom_call", output_to_operand_aliasing={{0}: (8, {}), {1}: (9, {})} | custom-call | bytes 14680064 | tf_op jit(solution)/shard_map/pallas_call | solution.py:87
  272.6 2.6 shard_map.110
  275.2 2.6 shard_map.111
  277.8 2.6 shard_map.112
  280.4 2.0 shard_map.113
  (64 shorter events, 10.6 us)
Async XLA Ops:
  3.4 15.6 %collective-permute-start = (bf16[256,1024]{1,0:T(8,128)(2,1)}, bf16[256,1024]{1,0:T(8,128)(2,1)}, u32[]{:S(2)}, u32[]{:S(2)}) collective-permute-start(bf16[256,1024]{1,0:T(8,128)(2,1)} %get-tuple-element.25.refs_0_), channel_id=1, source_target_pairs={{0,8},{8,0},{16,24},{24,16},{1,9},{9,1},{17,25},{25,17},{2,10},{10... | collective-permute-start | bytes 1572872 | tf_op jit(solution)/shard_map/ppermute | solution.py:105
  6.4 213.0 %copy-start.15 = (f32[128]{0:T(128)S(1)}, f32[128]{0:T(128)}, u32[]{:S(2)}) copy-start(f32[128]{0:T(128)} %param.14) | copy-start | bytes 1540
  6.4 213.0 %copy-start.16 = (f32[128]{0:T(128)S(1)}, f32[128]{0:T(128)}, u32[]{:S(2)}) copy-start(f32[128]{0:T(128)} %param.15) | copy-start | bytes 1540
  6.4 15.1 %collective-permute-start.2 = (bf16[256,1024]{1,0:T(8,128)(2,1)}, bf16[256,1024]{1,0:T(8,128)(2,1)}, u32[]{:S(2)}, u32[]{:S(2)}) collective-permute-start(bf16[256,1024]{1,0:T(8,128)(2,1)} %get-tuple-element.26.refs_4_), channel_id=1, source_target_pairs={{0,16},{8,24},{16,0},{24,8},{1,17},{9,25},{17,1},{25,9},{2,18},{10... | collective-permute-start | bytes 1572872 | tf_op jit(solution)/shard_map/ppermute | solution.py:105
  7.9 24.7 %collective-permute-start.16 = (bf16[256,1024]{1,0:T(8,128)(2,1)}, bf16[256,1024]{1,0:T(8,128)(2,1)S(1)}, u32[]{:S(2)}, u32[]{:S(2)}) collective-permute-start(bf16[256,1024]{1,0:T(8,128)(2,1)} %get-tuple-element.25.refs_0_), channel_id=1, source_target_pairs={{0,16},{8,24},{16,0},{24,8},{1,17},{9,25},{17,1},{25,9},{2,18},{10... | collective-permute-start | bytes 1572872 | tf_op jit(solution)/shard_map/ppermute | solution.py:105
  11.9 44.1 %collective-permute-start.10 = (bf16[512,1024]{1,0:T(8,128)(2,1)}, bf16[512,1024]{1,0:T(8,128)(2,1)S(1)}, u32[]{:S(2)}, u32[]{:S(2)}) collective-permute-start(bf16[512,1024]{1,0:T(8,128)(2,1)} %get-tuple-element.30.refs_6_), channel_id=1, source_target_pairs={{0,16},{8,24},{16,0},{24,8},{1,17},{9,25},{17,1},{25,9},{2,18},{10... | collective-permute-start | bytes 3145736 | tf_op jit(solution)/shard_map/ppermute | solution.py:105
  16.8 40.7 %collective-permute-start.12 = (bf16[512,1024]{1,0:T(8,128)(2,1)}, bf16[512,1024]{1,0:T(8,128)(2,1)}, u32[]{:S(2)}, u32[]{:S(2)}) collective-permute-start(bf16[512,1024]{1,0:T(8,128)(2,1)} %get-tuple-element.31.refs_1_), channel_id=1, source_target_pairs={{0,8},{8,0},{16,24},{24,16},{1,9},{9,1},{17,25},{25,17},{2,10},{10... | collective-permute-start | bytes 3145736 | tf_op jit(solution)/shard_map/ppermute | solution.py:105
  19.0 58.7 %collective-permute-start.14 = (bf16[512,1024]{1,0:T(8,128)(2,1)}, bf16[512,1024]{1,0:T(8,128)(2,1)}, u32[]{:S(2)}, u32[]{:S(2)}) collective-permute-start(bf16[512,1024]{1,0:T(8,128)(2,1)} %get-tuple-element.32.refs_5_), channel_id=1, source_target_pairs={{0,16},{8,24},{16,0},{24,8},{1,17},{9,25},{17,1},{25,9},{2,18},{10... | collective-permute-start | bytes 3145736 | tf_op jit(solution)/shard_map/ppermute | solution.py:105
  21.5 32.7 %collective-permute-start.17 = (bf16[256,1024]{1,0:T(8,128)(2,1)S(1)}, bf16[256,1024]{1,0:T(8,128)(2,1)S(1)}, u32[]{:S(2)}, u32[]{:S(2)}) collective-permute-start(bf16[256,1024]{1,0:T(8,128)(2,1)S(1)} %copy-done.14), channel_id=1, source_target_pairs={{0,8},{8,0},{16,24},{24,16},{1,9},{9,1},{17,25},{25,17},{2,10},{10... | collective-permute-start | bytes 1572872 | tf_op jit(solution)/shard_map/ppermute | solution.py:105
  33.5 44.3 %collective-permute-start.4 = (bf16[512,1024]{1,0:T(8,128)(2,1)}, bf16[512,1024]{1,0:T(8,128)(2,1)S(1)}, u32[]{:S(2)}, u32[]{:S(2)}) collective-permute-start(bf16[512,1024]{1,0:T(8,128)(2,1)} %get-tuple-element.27.refs_3_), channel_id=1, source_target_pairs={{0,8},{8,0},{16,24},{24,16},{1,9},{9,1},{17,25},{25,17},{2,10},{10... | collective-permute-start | bytes 3145736 | tf_op jit(solution)/shard_map/ppermute | solution.py:105
  55.1 45.0 %collective-permute-start.6 = (bf16[512,1024]{1,0:T(8,128)(2,1)}, bf16[512,1024]{1,0:T(8,128)(2,1)S(1)}, u32[]{:S(2)}, u32[]{:S(2)}) collective-permute-start(bf16[512,1024]{1,0:T(8,128)(2,1)} %get-tuple-element.28.refs_7_), channel_id=1, source_target_pairs={{0,16},{8,24},{16,0},{24,8},{1,17},{9,25},{17,1},{25,9},{2,18},{10... | collective-permute-start | bytes 3145736 | tf_op jit(solution)/shard_map/ppermute | solution.py:105
  56.0 205.0 %copy-start.2 = (bf16[512,1024]{1,0:T(8,128)(2,1)}, bf16[512,1024]{1,0:T(8,128)(2,1)S(1)}, u32[]{:S(2)}) copy-start(bf16[512,1024]{1,0:T(8,128)(2,1)S(1)} %collective-permute-done.10.refs_5_) | copy-start | bytes 3145732
  56.0 44.2 %collective-permute-start.8 = (bf16[512,1024]{1,0:T(8,128)(2,1)}, bf16[512,1024]{1,0:T(8,128)(2,1)}, u32[]{:S(2)}, u32[]{:S(2)}) collective-permute-start(bf16[512,1024]{1,0:T(8,128)(2,1)} %get-tuple-element.29.refs_2_), channel_id=1, source_target_pairs={{0,8},{8,0},{16,24},{24,16},{1,9},{9,1},{17,25},{25,17},{2,10},{10... | collective-permute-start | bytes 3145736 | tf_op jit(solution)/shard_map/ppermute | solution.py:105
  57.5 65.1 %collective-permute-start.18 = (bf16[512,1024]{1,0:T(8,128)(2,1)}, bf16[512,1024]{1,0:T(8,128)(2,1)S(1)}, u32[]{:S(2)}, u32[]{:S(2)}) collective-permute-start(bf16[512,1024]{1,0:T(8,128)(2,1)} %get-tuple-element.31.refs_1_), channel_id=1, source_target_pairs={{0,16},{8,24},{16,0},{24,8},{1,17},{9,25},{17,1},{25,9},{2,18},{10... | collective-permute-start | bytes 3145736 | tf_op jit(solution)/shard_map/ppermute | solution.py:105
  77.7 44.9 %collective-permute-start.19 = (bf16[512,1024]{1,0:T(8,128)(2,1)}, bf16[512,1024]{1,0:T(8,128)(2,1)S(1)}, u32[]{:S(2)}, u32[]{:S(2)}) collective-permute-start(bf16[512,1024]{1,0:T(8,128)(2,1)} %get-tuple-element.32.refs_5_), channel_id=1, source_target_pairs={{0,8},{8,0},{16,24},{24,16},{1,9},{9,1},{17,25},{25,17},{2,10},{10... | collective-permute-start | bytes 3145736 | tf_op jit(solution)/shard_map/ppermute | solution.py:105
  77.8 183.2 %copy-start = (bf16[512,1024]{1,0:T(8,128)(2,1)}, bf16[512,1024]{1,0:T(8,128)(2,1)S(1)}, u32[]{:S(2)}) copy-start(bf16[512,1024]{1,0:T(8,128)(2,1)S(1)} %collective-permute-done.4.refs_6_) | copy-start | bytes 3145732
  77.8 67.2 %collective-permute-start.20 = (bf16[512,1024]{1,0:T(8,128)(2,1)}, bf16[512,1024]{1,0:T(8,128)(2,1)S(1)}, u32[]{:S(2)}, u32[]{:S(2)}) collective-permute-start(bf16[512,1024]{1,0:T(8,128)(2,1)} %get-tuple-element.29.refs_2_), channel_id=1, source_target_pairs={{0,16},{8,24},{16,0},{24,8},{1,17},{9,25},{17,1},{25,9},{2,18},{10... | collective-permute-start | bytes 3145736 | tf_op jit(solution)/shard_map/ppermute | solution.py:105
  100.1 160.9 %copy-start.1 = (bf16[512,1024]{1,0:T(8,128)(2,1)}, bf16[512,1024]{1,0:T(8,128)(2,1)S(1)}, u32[]{:S(2)}) copy-start(bf16[512,1024]{1,0:T(8,128)(2,1)S(1)} %collective-permute-done.6.refs_7_) | copy-start | bytes 3145732
  100.1 45.0 %collective-permute-start.21 = (bf16[512,1024]{1,0:T(8,128)(2,1)}, bf16[512,1024]{1,0:T(8,128)(2,1)S(1)}, u32[]{:S(2)}, u32[]{:S(2)}) collective-permute-start(bf16[512,1024]{1,0:T(8,128)(2,1)} %get-tuple-element.30.refs_6_), channel_id=1, source_target_pairs={{0,8},{8,0},{16,24},{24,16},{1,9},{9,1},{17,25},{25,17},{2,10},{10... | collective-permute-start | bytes 3145736 | tf_op jit(solution)/shard_map/ppermute | solution.py:105
  100.2 67.3 %collective-permute-start.22 = (bf16[512,1024]{1,0:T(8,128)(2,1)}, bf16[512,1024]{1,0:T(8,128)(2,1)S(1)}, u32[]{:S(2)}, u32[]{:S(2)}) collective-permute-start(bf16[512,1024]{1,0:T(8,128)(2,1)} %get-tuple-element.27.refs_3_), channel_id=1, source_target_pairs={{0,16},{8,24},{16,0},{24,8},{1,17},{9,25},{17,1},{25,9},{2,18},{10... | collective-permute-start | bytes 3145736 | tf_op jit(solution)/shard_map/ppermute | solution.py:105
  122.5 89.0 %copy-start.3 = (bf16[512,1024]{1,0:T(8,128)(2,1)}, bf16[512,1024]{1,0:T(8,128)(2,1)S(1)}, u32[]{:S(2)}) copy-start(bf16[512,1024]{1,0:T(8,128)(2,1)S(1)} %collective-permute-done.18.refs_2_) | copy-start | bytes 3145732
  122.5 46.5 %collective-permute-start.23 = (bf16[512,1024]{1,0:T(8,128)(2,1)}, bf16[512,1024]{1,0:T(8,128)(2,1)S(1)}, u32[]{:S(2)}, u32[]{:S(2)}) collective-permute-start(bf16[512,1024]{1,0:T(8,128)(2,1)} %get-tuple-element.28.refs_7_), channel_id=1, source_target_pairs={{0,8},{8,0},{16,24},{24,16},{1,9},{9,1},{17,25},{25,17},{2,10},{10... | collective-permute-start | bytes 3145736 | tf_op jit(solution)/shard_map/ppermute | solution.py:105
  122.6 89.0 %copy-start.4 = (bf16[512,1024]{1,0:T(8,128)(2,1)}, bf16[512,1024]{1,0:T(8,128)(2,1)S(1)}, u32[]{:S(2)}) copy-start(bf16[512,1024]{1,0:T(8,128)(2,1)S(1)} %collective-permute-done.19.refs_3_) | copy-start | bytes 3145732
  122.6 67.3 %collective-permute-start.13 = (bf16[512,1024]{1,0:T(8,128)(2,1)}, bf16[512,1024]{1,0:T(8,128)(2,1)S(1)}, u32[]{:S(2)}, u32[]{:S(2)}) collective-permute-start(bf16[512,1024]{1,0:T(8,128)(2,1)} %collective-permute-done.12.refs_2_), channel_id=1, source_target_pairs={{0,16},{8,24},{16,0},{24,8},{1,17},{9,25},{17,1},{25,9},{2,18},{10... | collective-permute-start | bytes 3145736 | tf_op jit(solution)/shard_map/ppermute | solution.py:105
  145.0 66.6 %copy-start.5 = (bf16[512,1024]{1,0:T(8,128)(2,1)}, bf16[512,1024]{1,0:T(8,128)(2,1)S(1)}, u32[]{:S(2)}) copy-start(bf16[512,1024]{1,0:T(8,128)(2,1)S(1)} %collective-permute-done.20.refs_4_) | copy-start | bytes 3145732
  145.0 45.0 %collective-permute-start.15 = (bf16[512,1024]{1,0:T(8,128)(2,1)}, bf16[512,1024]{1,0:T(8,128)(2,1)S(1)}, u32[]{:S(2)}, u32[]{:S(2)}) collective-permute-start(bf16[512,1024]{1,0:T(8,128)(2,1)} %collective-permute-done.14.refs_3_), channel_id=1, source_target_pairs={{0,8},{8,0},{16,24},{24,16},{1,9},{9,1},{17,25},{25,17},{2,10},{10... | collective-permute-start | bytes 3145736 | tf_op jit(solution)/shard_map/ppermute | solution.py:105
  145.1 66.5 %collective-permute-start.11 = (bf16[512,1024]{1,0:T(8,128)(2,1)S(1)}, bf16[512,1024]{1,0:T(8,128)(2,1)S(1)}, u32[]{:S(2)}, u32[]{:S(2)}) collective-permute-start(bf16[512,1024]{1,0:T(8,128)(2,1)S(1)} %collective-permute-done.10.refs_5_), channel_id=1, source_target_pairs={{0,8},{8,0},{16,24},{24,16},{1,9},{9,1},{17,25},{25,17},{2,10},{10... | collective-permute-start | bytes 3145736 | tf_op jit(solution)/shard_map/ppermute | solution.py:105
  167.5 107.7 %collective-permute-start.9 = (bf16[512,1024]{1,0:T(8,128)(2,1)}, bf16[512,1024]{1,0:T(8,128)(2,1)}, u32[]{:S(2)}, u32[]{:S(2)}) collective-permute-start(bf16[512,1024]{1,0:T(8,128)(2,1)} %collective-permute-done.8.refs_4_), channel_id=1, source_target_pairs={{0,16},{8,24},{16,0},{24,8},{1,17},{9,25},{17,1},{25,9},{2,18},{10... | collective-permute-start | bytes 3145736 | tf_op jit(solution)/shard_map/ppermute | solution.py:105
  169.0 108.8 %collective-permute-start.5 = (bf16[512,1024]{1,0:T(8,128)(2,1)S(1)}, bf16[512,1024]{1,0:T(8,128)(2,1)}, u32[]{:S(2)}, u32[]{:S(2)}) collective-permute-start(bf16[512,1024]{1,0:T(8,128)(2,1)S(1)} %collective-permute-done.4.refs_6_), channel_id=1, source_target_pairs={{0,16},{8,24},{16,0},{24,8},{1,17},{9,25},{17,1},{25,9},{2,18},{10... | collective-permute-start | bytes 3145736 | tf_op jit(solution)/shard_map/ppermute | solution.py:105
  190.0 87.8 %collective-permute-start.7 = (bf16[512,1024]{1,0:T(8,128)(2,1)S(1)}, bf16[512,1024]{1,0:T(8,128)(2,1)}, u32[]{:S(2)}, u32[]{:S(2)}) collective-permute-start(bf16[512,1024]{1,0:T(8,128)(2,1)S(1)} %collective-permute-done.6.refs_7_), channel_id=1, source_target_pairs={{0,8},{8,0},{16,24},{24,16},{1,9},{9,1},{17,25},{25,17},{2,10},{10... | collective-permute-start | bytes 3145736 | tf_op jit(solution)/shard_map/ppermute | solution.py:105
  190.0 90.3 %collective-permute-start.1 = (bf16[256,1024]{1,0:T(8,128)(2,1)}, bf16[256,1024]{1,0:T(8,128)(2,1)}, u32[]{:S(2)}, u32[]{:S(2)}) collective-permute-start(bf16[256,1024]{1,0:T(8,128)(2,1)} %collective-permute-done.refs_0_), channel_id=1, source_target_pairs={{0,16},{8,24},{16,0},{24,8},{1,17},{9,25},{17,1},{25,9},{2,18},{10... | collective-permute-start | bytes 1572872 | tf_op jit(solution)/shard_map/ppermute | solution.py:105
  212.6 67.8 %collective-permute-start.3 = (bf16[256,1024]{1,0:T(8,128)(2,1)}, bf16[256,1024]{1,0:T(8,128)(2,1)}, u32[]{:S(2)}, u32[]{:S(2)}) collective-permute-start(bf16[256,1024]{1,0:T(8,128)(2,1)} %collective-permute-done.2.refs_1_), channel_id=1, source_target_pairs={{0,8},{8,0},{16,24},{24,16},{1,9},{9,1},{17,25},{25,17},{2,10},{10... | collective-permute-start | bytes 1572872 | tf_op jit(solution)/shard_map/ppermute | solution.py:105
  (9 other events, 217.2 us)
where the time goes:
time: 283 us; the launch traced here: 282 us
  waiting for transfers between devices  170 us (60%)
  blocking collectives  40.9 us (14%)
  Pallas kernels  40.3 us (14%)
  starting transfers between devices  27.1 us (10%)
    ppermute x24, waiting for transfers between devices, hop(): return lax.ppermute(piece, 'shard', perm=[(i, i ^ step) for i in range(n)])  170 us
    all_gather x1, blocking collectives, per_device(): lax.all_gather((norm_train + norm_step).astype(jnp.bfloat16), ('shard', '...  40.9 us
    pallas_call x7, Pallas kernels, place(): pl.pallas_call(functools.partial(place_body, jobs, aliased), in_specs=[an...  27.3 us
    ppermute x24, starting transfers between devices, hop(): return lax.ppermute(piece, 'shard', perm=[(i, i ^ step) for i in range(n)])  27.1 us
    pallas_call x4, Pallas kernels, merge(): pl.pallas_call(merge_body, grid=(size // TILE,), in_specs=in_specs, out_s...  13.1 us
  transfers between devices with their start and end apart: 24, of which 10 were waited for; matrix products, arithmetic and copies ran while one was open for 0% of the time, Pallas kernels for 13%

commit v1 on v0

--- a/solution.py
+++ b/solution.py
@@ -9,16 +9,18 @@
 
 
 mix_rate = 1.0
-TILE = 256
+TILE = 128
 GRANT = 60 << 20
+GROWTH = {1: 3, 3: 4}
 
 
 def chunks_of(width):
-    cuts, at = [], 0
+    cuts, at, tiles = [], 0, 1
     while at < width:
-        size = min(TILE if at == 0 else 2 * TILE, width - at)
+        size = min(tiles * TILE, width - at)
         cuts.append((at, size))
         at += size
+        tiles = GROWTH.get(tiles, 6)
     return cuts
 
 
@@ -34,17 +36,18 @@
 def merge(weights, start, size):
     train, low, _ = weights[0]
     rows, rank = train.shape[0], low.shape[0]
-    first = start // TILE
+    tile = 2 * TILE if start % (2 * TILE) == 0 and size % (2 * TILE) == 0 else TILE
+    first = start // tile
     in_specs = [
-        pl.BlockSpec((rows, TILE), lambda j: (0, first + j)),
+        pl.BlockSpec((rows, tile), lambda j: (0, first + j)),
         pl.BlockSpec((rank, rows), lambda j: (0, 0)),
-        pl.BlockSpec((rank, TILE), lambda j: (0, first + j)),
+        pl.BlockSpec((rank, tile), lambda j: (0, first + j)),
     ] * 2
     return pl.pallas_call(
         merge_body,
-        grid=(size // TILE,),
+        grid=(size // tile,),
         in_specs=in_specs,
-        out_specs=[pl.BlockSpec((TILE, rows), lambda j: (j, 0))] * 2,
+        out_specs=[pl.BlockSpec((tile, rows), lambda j: (j, 0))] * 2,
         out_shape=[jax.ShapeDtypeStruct((size, rows), jnp.bfloat16)] * 2,
         compiler_params=pltpu.CompilerParams(vmem_limit_bytes=GRANT),
         cost_estimate=pl.CostEstimate(
@@ -98,7 +101,7 @@
 
 
 def last_order(cuts):
-    return list(range(1, len(cuts))) + [0]
+    return list(range(len(cuts)))[::-1]
 
 
 def hop(n, step, piece):

time: 283 us -> 299 us (1.057)
  starting transfers between devices: 27.1 us -> 35.6 us
  waiting for transfers between devices: 170 us -> 175 us
    ppermute x24, starting transfers between devices: 27.1 us -> 35.6 us  [hop(): return lax.ppermute(piece, 'shard', perm=[(i, i ^ step) for i in range(n)])]
    ppermute x24, waiting for transfers between devices: 170 us -> 175 us  [hop(): return lax.ppermute(piece, 'shard', perm=[(i, i ^ step) for i in range(n)])]
  transfers between devices with their start and end apart: 24 -> 24, of which waited for: 10 -> 10; matrix products, arithmetic and copies ran while one was open for 0% -> 0% of each run, Pallas kernels for 13% -> 12%
where the time goes in v1:
time: 299 us; the launch traced here: 298 us
  waiting for transfers between devices  175 us (59%)
  Pallas kernels  42.8 us (14%)
  blocking collectives  40.9 us (14%)
  starting transfers between devices  35.6 us (12%)
  local copies, waits for them, and re-layouts  3.02 us (1%)
    ppermute x24, waiting for transfers between devices, hop(): return lax.ppermute(piece, 'shard', perm=[(i, i ^ step) for i in range(n)])  175 us
    all_gather x1, blocking collectives, per_device(): lax.all_gather((norm_train + norm_step).astype(jnp.bfloat16), ('shard', '...  40.9 us
    ppermute x24, starting transfers between devices, hop(): return lax.ppermute(piece, 'shard', perm=[(i, i ^ step) for i in range(n)])  35.6 us
    pallas_call x7, Pallas kernels, place(): pl.pallas_call(functools.partial(place_body, jobs, aliased), in_specs=[an...  27.8 us
    pallas_call x4, Pallas kernels, merge(): pl.pallas_call(merge_body, grid=(size // tile,), in_specs=in_specs, out_s...  15 us
  transfers between devices with their start and end apart: 24, of which 10 were waited for; matrix products, arithmetic and copies ran while one was open for 0% of the time, Pallas kernels for 12%

profile of v1, /device:TPU:0, one launch (start us, length us, event | category | flops | bytes accessed | tf_op | source)
XLA Modules:
  0.0 298.3 jit_solution(13788630227769633992)
XLA Ops:
  0.6 4.0 %shard_map.104 = (bf16[384,1024]{1,0:T(8,128)(2,1)}, bf16[384,1024]{1,0:T(8,128)(2,1)}) custom-call(bf16[1024,1792]{1,0:T(8,128)(2,1)} %refs_0_.7, bf16[32,1024]{1,0:T(8,128)(2,1)} %bitcast.5, bf16[32,1792]{1,0:T(8,128)(2,1)} %refs_2_.7, bf16[1024,1792]{1,0:T(8,128)(2,1)} %refs_3_.7, bf16[32,1024]{1,0:T(8,128)(2,1)} %bitcast.9, bf16[32,1792]{1,0:T(8,128)(2,1)} %refs_5_.7), custom_call_target="tpu_custom_call" | custom-call | flops 50331648 | bytes 3145728 | tf_op jit(solution)/shard_map/pallas_call | solution.py:46
  4.6 3.0 %collective-permute-start.4 = (bf16[384,1024]{1,0:T(8,128)(2,1)}, bf16[384,1024]{1,0:T(8,128)(2,1)S(1)}, u32[]{:S(2)}, u32[]{:S(2)}) collective-permute-start(bf16[384,1024]{1,0:T(8,128)(2,1)} %get-tuple-element.27.refs_1_), channel_id=1, source_target_pairs={{0,8},{8,0},{16,24},{24,16},{1,9},{9,1},{17,25},{25,17},{2,10},{10... | collective-permute-start | bytes 2359304 | tf_op jit(solution)/shard_map/ppermute | solution.py:108
  7.7 2.3 shard_map.103
  10.0 2.0 collective-permute-start.2
  12.1 2.0 collective-permute-start.6
  14.1 17.0 %collective-permute-done.refs_0_ = bf16[128,1024]{1,0:T(8,128)(2,1)S(1)} collective-permute-done((bf16[128,1024]{1,0:T(8,128)(2,1)}, bf16[128,1024]{1,0:T(8,128)(2,1)S(1)}, u32[]{:S(2)}, u32[]{:S(2)}) %collective-permute-start) | collective-permute-done | bytes 262176 | tf_op jit(solution)/shard_map/ppermute | solution.py:108
  34.8 3.4 %shard_map.105 = (bf16[512,1024]{1,0:T(8,128)(2,1)}, bf16[512,1024]{1,0:T(8,128)(2,1)}) custom-call(bf16[1024,1792]{1,0:T(8,128)(2,1)} %refs_0_.7, bf16[32,1024]{1,0:T(8,128)(2,1)} %bitcast.7, bf16[32,1792]{1,0:T(8,128)(2,1)} %refs_2_.7, bf16[1024,1792]{1,0:T(8,128)(2,1)} %refs_3_.7, bf16[32,1024]{1,0:T(8,128)(2,1)} %bitcast.11, bf16[32,1792]{1,0:T(8,128)(2,1)} %refs_5_.7), custom_call_target="tpu_custom_call" | custom-call | flops 67108864 | bytes 4194304 | tf_op jit(solution)/shard_map/pallas_call | solution.py:46
  38.2 2.2 collective-permute-done.17.refs_1_
  40.4 1.8 collective-permute-start.10
  44.2 5.3 %shard_map.106 = (bf16[768,1024]{1,0:T(8,128)(2,1)}, bf16[768,1024]{1,0:T(8,128)(2,1)}) custom-call(bf16[1024,1792]{1,0:T(8,128)(2,1)} %refs_0_.7, bf16[32,1024]{1,0:T(8,128)(2,1)} %bitcast.8, bf16[32,1792]{1,0:T(8,128)(2,1)} %refs_2_.7, bf16[1024,1792]{1,0:T(8,128)(2,1)} %refs_3_.7, bf16[32,1024]{1,0:T(8,128)(2,1)} %bitcast.12, bf16[32,1792]{1,0:T(8,128)(2,1)} %refs_5_.7), custom_call_target="tpu_custom_call" | custom-call | flops 100663296 | bytes 6291456 | tf_op jit(solution)/shard_map/pallas_call | solution.py:46
  49.5 9.2 %collective-permute-done.18.refs_2_ = bf16[384,1024]{1,0:T(8,128)(2,1)S(1)} collective-permute-done((bf16[384,1024]{1,0:T(8,128)(2,1)}, bf16[384,1024]{1,0:T(8,128)(2,1)S(1)}, u32[]{:S(2)}, u32[]{:S(2)}) %collective-permute-start.18) | collective-permute-done | bytes 786464 | tf_op jit(solution)/shard_map/ppermute | solution.py:108
  59.6 2.0 collective-permute-start.12
  64.0 17.3 %collective-permute-done.10.refs_5_ = bf16[512,1024]{1,0:T(8,128)(2,1)} collective-permute-done((bf16[512,1024]{1,0:T(8,128)(2,1)}, bf16[512,1024]{1,0:T(8,128)(2,1)}, u32[]{:S(2)}, u32[]{:S(2)}) %collective-permute-start.10) | collective-permute-done | bytes 1048608 | tf_op jit(solution)/shard_map/ppermute | solution.py:108
  81.3 2.0 collective-permute-start.21
  84.8 18.9 %collective-permute-done.20.refs_4_ = bf16[512,1024]{1,0:T(8,128)(2,1)} collective-permute-done((bf16[512,1024]{1,0:T(8,128)(2,1)}, bf16[512,1024]{1,0:T(8,128)(2,1)}, u32[]{:S(2)}, u32[]{:S(2)}) %collective-permute-start.20) | collective-permute-done | bytes 1048608 | tf_op jit(solution)/shard_map/ppermute | solution.py:108
  103.8 2.0 collective-permute-start.23
  105.8 30.1 %collective-permute-done.21.refs_5_ = bf16[512,1024]{1,0:T(8,128)(2,1)S(1)} collective-permute-done((bf16[512,1024]{1,0:T(8,128)(2,1)}, bf16[512,1024]{1,0:T(8,128)(2,1)S(1)}, u32[]{:S(2)}, u32[]{:S(2)}) %collective-permute-start.21) | collective-permute-done | bytes 1048608 | tf_op jit(solution)/shard_map/ppermute | solution.py:108
  135.9 1.7 collective-permute-start.11
  140.2 30.9 %collective-permute-done.22.refs_6_ = bf16[768,1024]{1,0:T(8,128)(2,1)S(1)} collective-permute-done((bf16[768,1024]{1,0:T(8,128)(2,1)}, bf16[768,1024]{1,0:T(8,128)(2,1)S(1)}, u32[]{:S(2)}, u32[]{:S(2)}) %collective-permute-start.22) | collective-permute-done | bytes 1572896 | tf_op jit(solution)/shard_map/ppermute | solution.py:108
  171.1 2.0 collective-permute-start.9
  173.2 18.9 %collective-permute-done.11.refs_1_ = bf16[512,1024]{1,0:T(8,128)(2,1)S(1)} collective-permute-done((bf16[512,1024]{1,0:T(8,128)(2,1)}, bf16[512,1024]{1,0:T(8,128)(2,1)S(1)}, u32[]{:S(2)}, u32[]{:S(2)}) %collective-permute-start.11) | collective-permute-done | bytes 1048608 | tf_op jit(solution)/shard_map/ppermute | solution.py:108
  193.8 10.9 %collective-permute-done.13.refs_0_ = bf16[768,1024]{1,0:T(8,128)(2,1)S(1)} collective-permute-done((bf16[768,1024]{1,0:T(8,128)(2,1)S(1)}, bf16[768,1024]{1,0:T(8,128)(2,1)S(1)}, u32[]{:S(2)}, u32[]{:S(2)}) %collective-permute-start.13) | collective-permute-done | bytes 1572896 | tf_op jit(solution)/shard_map/ppermute | solution.py:108
  204.8 2.0 collective-permute-start.1
  206.8 19.0 %collective-permute-done.15.refs_1_ = bf16[768,1024]{1,0:T(8,128)(2,1)S(1)} collective-permute-done((bf16[768,1024]{1,0:T(8,128)(2,1)S(1)}, bf16[768,1024]{1,0:T(8,128)(2,1)S(1)}, u32[]{:S(2)}, u32[]{:S(2)}) %collective-permute-start.15) | collective-permute-done | bytes 1572896 | tf_op jit(solution)/shard_map/ppermute | solution.py:108
  228.8 6.1 %shard_map.107 = (bf16[1792,4096]{1,0:T(8,128)(2,1)}, bf16[1792,4096]{1,0:T(8,128)(2,1)}) custom-call(bf16[128,1024]{1,0:T(8,128)(2,1)} %get-tuple-element.25.refs_0_, bf16[384,1024]{1,0:T(8,128)(2,1)} %get-tuple-element.27.refs_1_, bf16[512,1024]{1,0:T(8,128)(2,1)} %get-tuple-element.29.refs_2_, bf16[768,1024]{1,0:T(8,128)(2,1)} %get-tuple-element.31.refs_3_, ...), custom_call_target="tpu_custom_call" | custom-call | bytes 14680064 | tf_op jit(solution)/shard_map/pallas_call | solution.py:90
  234.9 40.9 %all-gather = bf16[32,1,128]{2,1,0:T(2,128)(2,1)S(1)} all-gather(bf16[1,1,128]{2,1,0:T(2,128)(2,1)S(1)} %convert_bitcast_fusion), channel_id=1, replica_groups=mesh['shard'=4,'cols'=8] {'shard','cols'}, dimensions={0}, use_global_device_ids=true | all-gather | bytes 8448 | tf_op jit(solution)/shard_map/all_gather | solution.py:144
  276.5 6.0 %shard_map.108 = (bf16[1792,4096]{1,0:T(8,128)(2,1)}, bf16[1792,4096]{1,0:T(8,128)(2,1)}) custom-call(bf16[128,1024]{1,0:T(8,128)(2,1)} %copy-done.12, bf16[128,1024]{1,0:T(8,128)(2,1)} %collective-permute-done.2.refs_1_, bf16[384,1024]{1,0:T(8,128)(2,1)} %copy-done.8, bf16[384,1024]{1,0:T(8,128)(2,1)} %copy-done.9, ...), custom_call_target="tpu_custom_call", output_to_operand_aliasing={{0}: (8, {}), {1}: (9, {})} | custom-call | bytes 14680064 | tf_op jit(solution)/shard_map/pallas_call | solution.py:90
  282.4 6.0 %shard_map.109 = (bf16[1792,4096]{1,0:T(8,128)(2,1)}, bf16[1792,4096]{1,0:T(8,128)(2,1)}) custom-call(bf16[128,1024]{1,0:T(8,128)(2,1)} %collective-permute-done.16.refs_0_, bf16[128,1024]{1,0:T(8,128)(2,1)} %copy-done.13, bf16[384,1024]{1,0:T(8,128)(2,1)} %copy-done.10, bf16[384,1024]{1,0:T(8,128)(2,1)} %copy-done.11, ...), custom_call_target="tpu_custom_call", output_to_operand_aliasing={{0}: (8, {}), {1}: (9, {})} | custom-call | bytes 14680064 | tf_op jit(solution)/shard_map/pallas_call | solution.py:90
  288.4 3.1 %shard_map.110 = (bf16[1792,4096]{1,0:T(8,128)(2,1)}, bf16[1792,4096]{1,0:T(8,128)(2,1)}) custom-call(bf16[768,1024]{1,0:T(8,128)(2,1)} %copy-done.4, bf16[768,1024]{1,0:T(8,128)(2,1)} %copy-done.5, bf16[1792,4096]{1,0:T(8,128)(2,1)} %get-tuple-element.37.refs_2_, ...), custom_call_target="tpu_custom_call", output_to_operand_aliasing={{0}: (2, {}), {1}: (3, {})} | custom-call | bytes 6291456 | tf_op jit(solution)/shard_map/pallas_call | solution.py:90
  291.5 2.6 shard_map.111
  294.2 2.3 shard_map.112
  296.5 1.8 shard_map.113
  (62 shorter events, 18.7 us)
Async XLA Ops:
  4.6 230.3 %copy-start.14 = (f32[128]{0:T(128)S(1)}, f32[128]{0:T(128)}, u32[]{:S(2)}) copy-start(f32[128]{0:T(128)} %param.14) | copy-start | bytes 1540
  4.6 230.3 %copy-start.15 = (f32[128]{0:T(128)S(1)}, f32[128]{0:T(128)}, u32[]{:S(2)}) copy-start(f32[128]{0:T(128)} %param.15) | copy-start | bytes 1540
  4.6 37.6 %collective-permute-start.4 = (bf16[384,1024]{1,0:T(8,128)(2,1)}, bf16[384,1024]{1,0:T(8,128)(2,1)S(1)}, u32[]{:S(2)}, u32[]{:S(2)}) collective-permute-start(bf16[384,1024]{1,0:T(8,128)(2,1)} %get-tuple-element.27.refs_1_), channel_id=1, source_target_pairs={{0,8},{8,0},{16,24},{24,16},{1,9},{9,1},{17,25},{25,17},{2,10},{10... | collective-permute-start | bytes 2359304 | tf_op jit(solution)/shard_map/ppermute | solution.py:108
  10.0 21.0 %collective-permute-start = (bf16[128,1024]{1,0:T(8,128)(2,1)}, bf16[128,1024]{1,0:T(8,128)(2,1)S(1)}, u32[]{:S(2)}, u32[]{:S(2)}) collective-permute-start(bf16[128,1024]{1,0:T(8,128)(2,1)} %get-tuple-element.25.refs_0_), channel_id=1, source_target_pairs={{0,8},{8,0},{16,24},{24,16},{1,9},{9,1},{17,25},{25,17},{2,10},{10... | collective-permute-start | bytes 786440 | tf_op jit(solution)/shard_map/ppermute | solution.py:108
  10.0 22.8 %collective-permute-start.2 = (bf16[128,1024]{1,0:T(8,128)(2,1)}, bf16[128,1024]{1,0:T(8,128)(2,1)}, u32[]{:S(2)}, u32[]{:S(2)}) collective-permute-start(bf16[128,1024]{1,0:T(8,128)(2,1)} %get-tuple-element.26.refs_4_), channel_id=1, source_target_pairs={{0,16},{8,24},{16,0},{24,8},{1,17},{9,25},{17,1},{25,9},{2,18},{10... | collective-permute-start | bytes 786440 | tf_op jit(solution)/shard_map/ppermute | solution.py:108
  12.0 22.3 %collective-permute-start.16 = (bf16[128,1024]{1,0:T(8,128)(2,1)}, bf16[128,1024]{1,0:T(8,128)(2,1)}, u32[]{:S(2)}, u32[]{:S(2)}) collective-permute-start(bf16[128,1024]{1,0:T(8,128)(2,1)} %get-tuple-element.25.refs_0_), channel_id=1, source_target_pairs={{0,16},{8,24},{16,0},{24,8},{1,17},{9,25},{17,1},{25,9},{2,18},{10... | collective-permute-start | bytes 786440 | tf_op jit(solution)/shard_map/ppermute | solution.py:108
  12.1 31.6 %collective-permute-start.6 = (bf16[384,1024]{1,0:T(8,128)(2,1)}, bf16[384,1024]{1,0:T(8,128)(2,1)S(1)}, u32[]{:S(2)}, u32[]{:S(2)}) collective-permute-start(bf16[384,1024]{1,0:T(8,128)(2,1)} %get-tuple-element.28.refs_5_), channel_id=1, source_target_pairs={{0,16},{8,24},{16,0},{24,8},{1,17},{9,25},{17,1},{25,9},{2,18},{10... | collective-permute-start | bytes 2359304 | tf_op jit(solution)/shard_map/ppermute | solution.py:108
  31.0 245.5 %copy-start.12 = (bf16[128,1024]{1,0:T(8,128)(2,1)}, bf16[128,1024]{1,0:T(8,128)(2,1)S(1)}, u32[]{:S(2)}) copy-start(bf16[128,1024]{1,0:T(8,128)(2,1)S(1)} %collective-permute-done.refs_0_) | copy-start | bytes 786436
  31.0 9.4 %collective-permute-start.17 = (bf16[128,1024]{1,0:T(8,128)(2,1)}, bf16[128,1024]{1,0:T(8,128)(2,1)S(1)}, u32[]{:S(2)}, u32[]{:S(2)}) collective-permute-start(bf16[128,1024]{1,0:T(8,128)(2,1)} %get-tuple-element.26.refs_4_), channel_id=1, source_target_pairs={{0,8},{8,0},{16,24},{24,16},{1,9},{9,1},{17,25},{25,17},{2,10},{10... | collective-permute-start | bytes 786440 | tf_op jit(solution)/shard_map/ppermute | solution.py:108
  32.8 25.9 %collective-permute-start.18 = (bf16[384,1024]{1,0:T(8,128)(2,1)}, bf16[384,1024]{1,0:T(8,128)(2,1)S(1)}, u32[]{:S(2)}, u32[]{:S(2)}) collective-permute-start(bf16[384,1024]{1,0:T(8,128)(2,1)} %get-tuple-element.27.refs_1_), channel_id=1, source_target_pairs={{0,16},{8,24},{16,0},{24,8},{1,17},{9,25},{17,1},{25,9},{2,18},{10... | collective-permute-start | bytes 2359304 | tf_op jit(solution)/shard_map/ppermute | solution.py:108
  34.3 27.3 %collective-permute-start.19 = (bf16[384,1024]{1,0:T(8,128)(2,1)}, bf16[384,1024]{1,0:T(8,128)(2,1)S(1)}, u32[]{:S(2)}, u32[]{:S(2)}) collective-permute-start(bf16[384,1024]{1,0:T(8,128)(2,1)} %get-tuple-element.28.refs_5_), channel_id=1, source_target_pairs={{0,8},{8,0},{16,24},{24,16},{1,9},{9,1},{17,25},{25,17},{2,10},{10... | collective-permute-start | bytes 2359304 | tf_op jit(solution)/shard_map/ppermute | solution.py:108
  40.4 40.9 %collective-permute-start.10 = (bf16[512,1024]{1,0:T(8,128)(2,1)}, bf16[512,1024]{1,0:T(8,128)(2,1)}, u32[]{:S(2)}, u32[]{:S(2)}) collective-permute-start(bf16[512,1024]{1,0:T(8,128)(2,1)} %get-tuple-element.30.refs_6_), channel_id=1, source_target_pairs={{0,16},{8,24},{16,0},{24,8},{1,17},{9,25},{17,1},{25,9},{2,18},{10... | collective-permute-start | bytes 3145736 | tf_op jit(solution)/shard_map/ppermute | solution.py:108
  42.2 41.1 %collective-permute-start.8 = (bf16[512,1024]{1,0:T(8,128)(2,1)}, bf16[512,1024]{1,0:T(8,128)(2,1)}, u32[]{:S(2)}, u32[]{:S(2)}) collective-permute-start(bf16[512,1024]{1,0:T(8,128)(2,1)} %get-tuple-element.29.refs_2_), channel_id=1, source_target_pairs={{0,8},{8,0},{16,24},{24,16},{1,9},{9,1},{17,25},{25,17},{2,10},{10... | collective-permute-start | bytes 3145736 | tf_op jit(solution)/shard_map/ppermute | solution.py:108
  43.7 60.1 %collective-permute-start.20 = (bf16[512,1024]{1,0:T(8,128)(2,1)}, bf16[512,1024]{1,0:T(8,128)(2,1)}, u32[]{:S(2)}, u32[]{:S(2)}) collective-permute-start(bf16[512,1024]{1,0:T(8,128)(2,1)} %get-tuple-element.29.refs_2_), channel_id=1, source_target_pairs={{0,16},{8,24},{16,0},{24,8},{1,17},{9,25},{17,1},{25,9},{2,18},{10... | collective-permute-start | bytes 3145736 | tf_op jit(solution)/shard_map/ppermute | solution.py:108
  59.6 78.0 %collective-permute-start.12 = (bf16[768,1024]{1,0:T(8,128)(2,1)}, bf16[768,1024]{1,0:T(8,128)(2,1)S(1)}, u32[]{:S(2)}, u32[]{:S(2)}) collective-permute-start(bf16[768,1024]{1,0:T(8,128)(2,1)} %get-tuple-element.31.refs_3_), channel_id=1, source_target_pairs={{0,8},{8,0},{16,24},{24,16},{1,9},{9,1},{17,25},{25,17},{2,10},{10... | collective-permute-start | bytes 4718600 | tf_op jit(solution)/shard_map/ppermute | solution.py:108
  62.5 76.7 %collective-permute-start.14 = (bf16[768,1024]{1,0:T(8,128)(2,1)}, bf16[768,1024]{1,0:T(8,128)(2,1)S(1)}, u32[]{:S(2)}, u32[]{:S(2)}) collective-permute-start(bf16[768,1024]{1,0:T(8,128)(2,1)} %get-tuple-element.32.refs_7_), channel_id=1, source_target_pairs={{0,16},{8,24},{16,0},{24,8},{1,17},{9,25},{17,1},{25,9},{2,18},{10... | collective-permute-start | bytes 4718600 | tf_op jit(solution)/shard_map/ppermute | solution.py:108
  81.3 54.6 %collective-permute-start.21 = (bf16[512,1024]{1,0:T(8,128)(2,1)}, bf16[512,1024]{1,0:T(8,128)(2,1)S(1)}, u32[]{:S(2)}, u32[]{:S(2)}) collective-permute-start(bf16[512,1024]{1,0:T(8,128)(2,1)} %get-tuple-element.30.refs_6_), channel_id=1, source_target_pairs={{0,8},{8,0},{16,24},{24,16},{1,9},{9,1},{17,25},{25,17},{2,10},{10... | collective-permute-start | bytes 3145736 | tf_op jit(solution)/shard_map/ppermute | solution.py:108
  83.3 87.8 %collective-permute-start.22 = (bf16[768,1024]{1,0:T(8,128)(2,1)}, bf16[768,1024]{1,0:T(8,128)(2,1)S(1)}, u32[]{:S(2)}, u32[]{:S(2)}) collective-permute-start(bf16[768,1024]{1,0:T(8,128)(2,1)} %get-tuple-element.31.refs_3_), channel_id=1, source_target_pairs={{0,16},{8,24},{16,0},{24,8},{1,17},{9,25},{17,1},{25,9},{2,18},{10... | collective-permute-start | bytes 4718600 | tf_op jit(solution)/shard_map/ppermute | solution.py:108
  103.8 69.3 %collective-permute-start.23 = (bf16[768,1024]{1,0:T(8,128)(2,1)}, bf16[768,1024]{1,0:T(8,128)(2,1)S(1)}, u32[]{:S(2)}, u32[]{:S(2)}) collective-permute-start(bf16[768,1024]{1,0:T(8,128)(2,1)} %get-tuple-element.32.refs_7_), channel_id=1, source_target_pairs={{0,8},{8,0},{16,24},{24,16},{1,9},{9,1},{17,25},{25,17},{2,10},{10... | collective-permute-start | bytes 4718600 | tf_op jit(solution)/shard_map/ppermute | solution.py:108
  135.9 56.2 %collective-permute-start.11 = (bf16[512,1024]{1,0:T(8,128)(2,1)}, bf16[512,1024]{1,0:T(8,128)(2,1)S(1)}, u32[]{:S(2)}, u32[]{:S(2)}) collective-permute-start(bf16[512,1024]{1,0:T(8,128)(2,1)} %collective-permute-done.10.refs_5_), channel_id=1, source_target_pairs={{0,8},{8,0},{16,24},{24,16},{1,9},{9,1},{17,25},{25,17},{2,10},{10... | collective-permute-start | bytes 3145736 | tf_op jit(solution)/shard_map/ppermute | solution.py:108
  137.7 138.8 %copy-start = (bf16[768,1024]{1,0:T(8,128)(2,1)}, bf16[768,1024]{1,0:T(8,128)(2,1)S(1)}, u32[]{:S(2)}) copy-start(bf16[768,1024]{1,0:T(8,128)(2,1)S(1)} %collective-permute-done.12.refs_6_) | copy-start | bytes 4718596
  137.7 67.1 %collective-permute-start.13 = (bf16[768,1024]{1,0:T(8,128)(2,1)S(1)}, bf16[768,1024]{1,0:T(8,128)(2,1)S(1)}, u32[]{:S(2)}, u32[]{:S(2)}) collective-permute-start(bf16[768,1024]{1,0:T(8,128)(2,1)S(1)} %collective-permute-done.12.refs_6_), channel_id=1, source_target_pairs={{0,16},{8,24},{16,0},{24,8},{1,17},{9,25},{17,1},{25,9},{2,18},{10... | collective-permute-start | bytes 4718600 | tf_op jit(solution)/shard_map/ppermute | solution.py:108
  139.2 137.2 %copy-start.1 = (bf16[768,1024]{1,0:T(8,128)(2,1)}, bf16[768,1024]{1,0:T(8,128)(2,1)S(1)}, u32[]{:S(2)}) copy-start(bf16[768,1024]{1,0:T(8,128)(2,1)S(1)} %collective-permute-done.14.refs_7_) | copy-start | bytes 4718596
  139.2 86.5 %collective-permute-start.15 = (bf16[768,1024]{1,0:T(8,128)(2,1)S(1)}, bf16[768,1024]{1,0:T(8,128)(2,1)S(1)}, u32[]{:S(2)}, u32[]{:S(2)}) collective-permute-start(bf16[768,1024]{1,0:T(8,128)(2,1)S(1)} %collective-permute-done.14.refs_7_), channel_id=1, source_target_pairs={{0,8},{8,0},{16,24},{24,16},{1,9},{9,1},{17,25},{25,17},{2,10},{10... | collective-permute-start | bytes 4718600 | tf_op jit(solution)/shard_map/ppermute | solution.py:108
  171.1 54.7 %copy-start.2 = (bf16[768,1024]{1,0:T(8,128)(2,1)}, bf16[768,1024]{1,0:T(8,128)(2,1)S(1)}, u32[]{:S(2)}) copy-start(bf16[768,1024]{1,0:T(8,128)(2,1)S(1)} %collective-permute-done.22.refs_6_) | copy-start | bytes 4718596
  171.1 120.5 %collective-permute-start.9 = (bf16[512,1024]{1,0:T(8,128)(2,1)}, bf16[512,1024]{1,0:T(8,128)(2,1)}, u32[]{:S(2)}, u32[]{:S(2)}) collective-permute-start(bf16[512,1024]{1,0:T(8,128)(2,1)} %collective-permute-done.8.refs_4_), channel_id=1, source_target_pairs={{0,16},{8,24},{16,0},{24,8},{1,17},{9,25},{17,1},{25,9},{2,18},{10... | collective-permute-start | bytes 3145736 | tf_op jit(solution)/shard_map/ppermute | solution.py:108
  173.1 52.7 %copy-start.3 = (bf16[768,1024]{1,0:T(8,128)(2,1)}, bf16[768,1024]{1,0:T(8,128)(2,1)S(1)}, u32[]{:S(2)}) copy-start(bf16[768,1024]{1,0:T(8,128)(2,1)S(1)} %collective-permute-done.23.refs_7_) | copy-start | bytes 4718596
  173.1 121.0 %collective-permute-start.5 = (bf16[384,1024]{1,0:T(8,128)(2,1)}, bf16[384,1024]{1,0:T(8,128)(2,1)}, u32[]{:S(2)}, u32[]{:S(2)}) collective-permute-start(bf16[384,1024]{1,0:T(8,128)(2,1)} %copy-done.8), channel_id=1, source_target_pairs={{0,16},{8,24},{16,0},{24,8},{1,17},{9,25},{17,1},{25,9},{2,18},{10... | collective-permute-start | bytes 2359304 | tf_op jit(solution)/shard_map/ppermute | solution.py:108
  192.1 33.7 %copy-start.7 = (bf16[512,1024]{1,0:T(8,128)(2,1)}, bf16[512,1024]{1,0:T(8,128)(2,1)S(1)}, u32[]{:S(2)}) copy-start(bf16[512,1024]{1,0:T(8,128)(2,1)S(1)} %collective-permute-done.11.refs_1_) | copy-start | bytes 3145732
  192.1 102.1 %collective-permute-start.7 = (bf16[384,1024]{1,0:T(8,128)(2,1)}, bf16[384,1024]{1,0:T(8,128)(2,1)}, u32[]{:S(2)}, u32[]{:S(2)}) collective-permute-start(bf16[384,1024]{1,0:T(8,128)(2,1)} %copy-done.9), channel_id=1, source_target_pairs={{0,8},{8,0},{16,24},{24,16},{1,9},{9,1},{17,25},{25,17},{2,10},{10... | collective-permute-start | bytes 2359304 | tf_op jit(solution)/shard_map/ppermute | solution.py:108
  204.8 91.7 %collective-permute-start.1 = (bf16[128,1024]{1,0:T(8,128)(2,1)S(1)}, bf16[128,1024]{1,0:T(8,128)(2,1)}, u32[]{:S(2)}, u32[]{:S(2)}) collective-permute-start(bf16[128,1024]{1,0:T(8,128)(2,1)S(1)} %collective-permute-done.refs_0_), channel_id=1, source_target_pairs={{0,16},{8,24},{16,0},{24,8},{1,17},{9,25},{17,1},{25,9},{2,18},{10... | collective-permute-start | bytes 786440 | tf_op jit(solution)/shard_map/ppermute | solution.py:108
  227.0 69.5 %collective-permute-start.3 = (bf16[128,1024]{1,0:T(8,128)(2,1)}, bf16[128,1024]{1,0:T(8,128)(2,1)}, u32[]{:S(2)}, u32[]{:S(2)}) collective-permute-start(bf16[128,1024]{1,0:T(8,128)(2,1)} %collective-permute-done.2.refs_1_), channel_id=1, source_target_pairs={{0,8},{8,0},{16,24},{24,16},{1,9},{9,1},{17,25},{25,17},{2,10},{10... | collective-permute-start | bytes 786440 | tf_op jit(solution)/shard_map/ppermute | solution.py:108
  (8 other events, 78.5 us)
